TPU v7x, 32 devices: a whole 2x2x4 slice. The times are simulated.
32 devices in a mesh: groups: 2 (over x), blk: 8 (over z, y), heads: 2 (over core).
Axes of the slice: x: 2, y: 2, z: 4, core: 2. Of those that a mesh axis runs over, the one named last changes fastest.
Arguments:
- image_feats: bfloat16 [4096, 8192], P(('groups', 'blk')), parts along dimension 0, may hold values from -6 to 6
- slot_image: int32 [4096], P(('groups', 'blk')), parts along dimension 0, may hold values from -1 to 3, as said below
- key_weight: bfloat16 [8192, 512], P('blk', 'heads'), may hold values from -0.0625 to 0.0625
- value_weight: bfloat16 [8192, 512], P('blk', 'heads'), may hold values from -0.0625 to 0.0625
- key_gain: float32 [128], replicated, may hold values from 0.25 to 1.75
- queries: bfloat16 [512, 4096], P(('groups', 'blk'), 'heads'), parts along dimension 0, may hold values from -60 to 60
- text_image: int32 [512], P('groups'), parts along dimension 0, may hold values from 0 to 3
- text_hidden: bfloat16 [512, 8192], P(('groups', 'heads'), 'blk'), parts along dimension 0, may hold values from -4 to 4
- out_weight: bfloat16 [4096, 8192], P('heads', 'blk'), may hold values from -0.09375 to 0.09375
- attn_gate: float32 [1], replicated, may hold values from 0.4 to 1.2
Outputs:
- mixed: bfloat16 [512, 8192], P(('groups', 'heads'), 'blk'), parts along dimension 0
There are 2 independent parts, one for each index of `groups`. A program takes and returns all parts, laid end to end along the dimension named above; an argument that names none is the same for every part. Nothing has to cross between parts.
Inputs may be any that keep to these rules, and one draw needn't show every extreme that they name: `slot_image`: slots come in tiles of 64; the live slots of a tile come first and carry one image id, -1 marks an empty slot; every image has live slots; the first 256 slots are all live.
All inputs are finite; a program needn't handle non-finite values.
Results may differ from a plain program's by a relative error of at most 0.008.
Values may be sent and summed in bfloat16 or wider, within the bound.
A program may use at most 128 MiB of HBM per device.

v0:
```python
import math

import jax
import jax.numpy as jnp
from jax import lax
from jax.sharding import PartitionSpec as P

HD = 128


def body(
    image_feats,
    slot_image,
    key_weight,
    value_weight,
    key_gain,
    queries,
    text_image,
    text_hidden,
    out_weight,
    attn_gate,
):
    tok_rows = image_feats.shape[0]
    kv_cols = key_weight.shape[1]
    kv_local = kv_cols // HD
    q_cols = queries.shape[1]
    q_per_kv = q_cols // kv_cols
    text_rows = queries.shape[0]
    score_scale = 1.0 / math.sqrt(HD)
    keys_raw = jnp.dot(
        image_feats,
        lax.all_gather(key_weight, "blk", axis=0, tiled=True),
        preferred_element_type=jnp.float32,
    )
    values_raw = jnp.dot(
        image_feats,
        lax.all_gather(value_weight, "blk", axis=0, tiled=True),
        preferred_element_type=jnp.float32,
    )
    key_heads_raw = keys_raw.reshape(tok_rows, kv_local, HD)
    norm_scale = lax.rsqrt(jnp.mean(key_heads_raw * key_heads_raw, axis=-1, keepdims=True) + 1e-05)
    keys = (key_heads_raw * norm_scale * key_gain).astype(jnp.bfloat16).reshape(tok_rows, kv_cols)
    values = values_raw.astype(jnp.bfloat16)
    row_start = lax.axis_index("blk") * text_rows
    row_images = lax.dynamic_slice_in_dim(text_image, row_start, text_rows, 0).astype(jnp.float32)
    query_heads = queries.reshape(text_rows, kv_local, q_per_kv, HD)
    slot_code = slot_image.astype(jnp.bfloat16)
    row_top = jnp.full((text_rows, kv_local, q_per_kv), -1e30, jnp.float32)
    piece_keys = lax.all_gather(keys, "blk", axis=0, tiled=True)
    piece_values = lax.all_gather(values, "blk", axis=0, tiled=True)
    attend_slot_code = lax.all_gather(slot_code, "blk", axis=0, tiled=True)
    count_rows = piece_keys.shape[0]
    slot_float = attend_slot_code.astype(jnp.float32)
    visible = (slot_float[None, :] >= 0.0) & (slot_float[None, :] <= row_images[:, None])
    visible_four = visible[:, None, None, :]
    key_heads = piece_keys.reshape(count_rows, kv_local, HD)
    value_heads = piece_values.reshape(count_rows, kv_local, HD)
    scores = (
        jnp.einsum("rgjd,sgd->rgjs", query_heads, key_heads, preferred_element_type=jnp.float32)
        * score_scale
    )
    masked_scores = jnp.where(visible_four, scores, -1e30)
    next_top = jnp.maximum(row_top, jnp.max(masked_scores, axis=-1))
    expo = jnp.where(visible_four, jnp.exp(scores - next_top[..., None]), 0.0)
    next_total = jnp.sum(expo, axis=-1)
    next_acc = jnp.einsum(
        "rgjs,sgd->rgjd", expo.astype(jnp.bfloat16), value_heads, preferred_element_type=jnp.float32
    )
    attn = (next_acc / next_total[..., None]).astype(jnp.bfloat16).reshape(text_rows, q_cols)
    partial_out = jnp.dot(
        lax.all_gather(attn, "blk", axis=0, tiled=True),
        out_weight,
        preferred_element_type=jnp.float32,
    )
    head_total = lax.psum_scatter(
        partial_out.astype(jnp.bfloat16), "heads", scatter_dimension=0, tiled=True
    ).astype(jnp.float32)
    return (text_hidden.astype(jnp.float32) + jnp.tanh(attn_gate[0]) * head_total).astype(
        jnp.bfloat16
    )


def solution(mesh):
    placed = (
        P(("groups", "blk"), None),
        P(("groups", "blk")),
        P("blk", "heads"),
        P("blk", "heads"),
        P(),
        P(("groups", "blk"), "heads"),
        P("groups"),
        P(("groups", "heads"), "blk"),
        P("heads", "blk"),
        P(),
    )
    return jax.shard_map(
        body, mesh=mesh, in_specs=placed, out_specs=P(("groups", "heads"), "blk"), check_vma=False
    )
```

profile of v0, /device:TPU:1, one launch (start us, length us, event | category | flops | bytes accessed | tf_op | source)
XLA Modules:
  0.0 303.9 jit_solution(10362841615920033740)
XLA Ops:
  6.5 0.7 all-gather.11.cloned.1.call-update
  7.3 0.0 all-gather.7.cloned.1.call-start
  7.3 0.7 all-gather.7.cloned.1.call-update
  8.0 0.0 all-gather.13.cloned.1.call-start
  8.1 75.1 %all-gather.11.cloned.1.call-done = bf16[8192,256]{1,0:T(8,128)(2,1)} async-done(((bf16[1024,256]{1,0:T(8,128)(2,1)}), bf16[8192,256]{1,0:T(8,128)(2,1)}) %all-gather.11.cloned.1.call-update) | async-done | bytes 4194320 | tf_op jit(solution)/shard_map/all_gather | solution.py:32
  83.1 5.2 %bitcast_reduce_fusion = (f32[256,2]{0,1:T(2,128)S(1)}, f32[256,256]{0,1:T(8,128)S(1)}) fusion(bf16[256,8192]{1,0:T(8,128)(2,1)} %param.10, bf16[8192,256]{1,0:T(8,128)(2,1)} %all-gather.11.cloned.1.call-done), kind=kOutput, calls=%fused_computation.19 | convolution fusion | flops 1073872384 | bytes 8652800 | tf_op jit(solution)/shard_map/dot_general | solution.py:30
  88.4 0.8 fusion.19
  89.1 0.0 all-gather.13.cloned.1.call-update
  89.2 0.0 all-gather.9.cloned.1.call-start
  89.2 67.4 %all-gather.7.cloned.1.call-done = bf16[8192,256]{1,0:T(8,128)(2,1)} async-done(((bf16[1024,256]{1,0:T(8,128)(2,1)}), bf16[8192,256]{1,0:T(8,128)(2,1)}) %all-gather.7.cloned.1.call-update) | async-done | bytes 4194320 | tf_op jit(solution)/shard_map/all_gather | solution.py:37
  156.6 5.4 %convolution_convert_fusion.1 = bf16[256,256]{1,0:T(8,128)(2,1)} fusion(bf16[256,8192]{1,0:T(8,128)(2,1)} %param.10, bf16[8192,256]{1,0:T(8,128)(2,1)} %all-gather.7.cloned.1.call-done), kind=kOutput, calls=%fused_computation.11 | convolution fusion | flops 1073807360 | bytes 8519680 | tf_op jit(solution)/shard_map/dot_general | solution.py:35
  162.0 0.0 all-gather.9.cloned.1.call-update
  162.0 0.0 all-gather.15.cloned.1.call-start
  162.1 15.6 %all-gather = bf16[8,1,256]{2,1,0:T(2,128)(2,1)S(1)} all-gather(bf16[1,1,256]{2,1,0:T(2,128)(2,1)S(1)} %reshape.71), channel_id=1, replica_groups=mesh['groups'=2,'blk'=8,'heads'=2] {'blk'}, dimensions={0}, use_global_device_ids=true | all-gather | bytes 4608 | tf_op jit(solution)/shard_map/all_gather | solution.py:51
  177.7 0.1 dynamic-slice_convert_fusion
  177.8 0.1 compare_and_fusion
  177.9 17.4 %all-gather.13.cloned.1.call-done = bf16[2048,256]{0,1:T(8,128)(2,1)} async-done(((bf16[256,256]{0,1:T(8,128)(2,1)}), bf16[2048,256]{0,1:T(8,128)(2,1)}) %all-gather.13.cloned.1.call-update) | async-done | bytes 1048592 | tf_op jit(solution)/shard_map/all_gather | solution.py:49
  195.4 2.1 fusion
  197.5 1.9 copy-done.1
  199.5 1.1 fusion.3
  200.5 37.0 %all-gather.9.cloned.1.call-done = bf16[2048,256]{1,0:T(8,128)(2,1)} async-done(((bf16[256,256]{1,0:T(8,128)(2,1)}), bf16[2048,256]{1,0:T(8,128)(2,1)}) %all-gather.9.cloned.1.call-update) | async-done | bytes 1048592 | tf_op jit(solution)/shard_map/all_gather | solution.py:50
  237.5 1.3 reshape.67
  238.8 3.1 %fusion.14 = bf16[32,2,8,128]{3,0,2,1:T(8,128)(2,1)S(1)} fusion(f32[2,2048,32,8]{1,2,3,0:T(8,128)} %copy-done.1, f32[32,2,8]{0,2,1:T(8,128)S(1)} %broadcast_maximum_fusion, pred[32,2048]{1,0:T(8,128)(4,1)S(1)} %compare_and_fusion, bf16[2048,2,128,1]{2,1,0,3:T(2,128)(2,1)S(1)} %bitcast.60, f32[32,2,8]{0,2,1:T(8,128)S(1)} %fusion.3), kind=kOutput, calls=%fused_computation.13 | convolution fusion | flops 272760832 | bytes 5443584 | tf_op jit(solution)/shard_map/rgjs,sgd->rgjd/dot_general | solution.py:66
  241.9 0.1 copy.21
  242.0 0.7 copy.37
  242.7 0.0 all-gather.15.cloned.1.call-update
  242.7 0.0 reduce-scatter.2.cloned.1.call-start
  242.7 39.1 %all-gather.15.cloned.1.call-done = bf16[256,2048]{1,0:T(8,128)(2,1)} async-done(((bf16[32,2048]{1,0:T(8,128)(2,1)}), bf16[256,2048]{1,0:T(8,128)(2,1)}) %all-gather.15.cloned.1.call-update) | async-done | bytes 1048592 | tf_op jit(solution)/shard_map/all_gather | solution.py:71
  281.8 4.6 %convolution_convert_fusion = bf16[256,1024]{1,0:T(8,128)(2,1)} fusion(bf16[256,2048]{1,0:T(8,128)(2,1)} %all-gather.15.cloned.1.call-done, bf16[2048,1024]{1,0:T(8,128)(2,1)} %param.18), kind=kOutput, calls=%fused_computation.9 | convolution fusion | flops 1074003968 | bytes 5767168 | tf_op jit(solution)/shard_map/dot_general | solution.py:70
  286.4 0.0 reduce-scatter.2.cloned.1.call-update
  287.1 8.1 %reduce-scatter.2.cloned.1.call-done = bf16[128,1024]{1,0:T(8,128)(2,1)} async-done(((bf16[256,1024]{1,0:T(8,128)(2,1)}), bf16[128,1024]{1,0:T(8,128)(2,1)}) %reduce-scatter.2.cloned.1.call-update) | async-done | bytes 262160 | tf_op jit(solution)/shard_map/reduce_scatter | solution.py:75
  295.3 1.8 add_convert_fusion
  (20 shorter events, 0.1 us)
Async XLA Ops:
  6.5 1.5 copy-start
  6.5 76.6 %all-gather.11.cloned.1.call-start = ((), (), s32[]{:S(2)}) async-start(), calls=%async_computation.3 | async-start | bytes 4718592 | tf_op jit(solution)/shard_map/all_gather | solution.py:32
  7.3 149.4 %all-gather.7.cloned.1.call-start = ((), (), s32[]{:S(2)}) async-start(), calls=%async_computation.1 | async-start | bytes 4718592 | tf_op jit(solution)/shard_map/all_gather | solution.py:37
  8.0 187.4 %all-gather.13.cloned.1.call-start = ((), (), s32[]{:S(2)}) async-start(), calls=%async_computation.4 | async-start | bytes 1179648 | tf_op jit(solution)/shard_map/all_gather | solution.py:49
  89.2 72.9 %copy-start.4 = (s32[256]{0:T(256)S(1)}, s32[256]{0:T(256)}, u32[]{:S(2)}) copy-start(s32[256]{0:T(256)} %param.11) | copy-start | bytes 3076
  89.2 88.5 %copy-start.3 = (bf16[32,2048]{1,0:T(8,128)(2,1)S(1)}, bf16[32,2048]{1,0:T(8,128)(2,1)}, u32[]{:S(2)}) copy-start(bf16[32,2048]{1,0:T(8,128)(2,1)} %param.15) | copy-start | bytes 393220
  89.2 88.5 %copy-start.5 = (s32[256]{0:T(256)S(1)}, s32[256]{0:T(256)}, u32[]{:S(2)}) copy-start(s32[256]{0:T(256)} %param.16) | copy-start | bytes 3076
  89.2 148.3 %all-gather.9.cloned.1.call-start = ((), (), s32[]{:S(2)}) async-start(), calls=%async_computation.2 | async-start | bytes 1179648 | tf_op jit(solution)/shard_map/all_gather | solution.py:50
  162.0 119.8 %all-gather.15.cloned.1.call-start = ((), (), s32[]{:S(2)}) async-start(), calls=%async_computation.5 | async-start | bytes 1179648 | tf_op jit(solution)/shard_map/all_gather | solution.py:71
  197.5 2.0 copy-start.1
  242.0 53.3 %copy-start.2 = (bf16[128,1024]{1,0:T(8,128)(2,1)S(1)}, bf16[128,1024]{1,0:T(8,128)(2,1)}, u32[]{:S(2)}) copy-start(bf16[128,1024]{1,0:T(8,128)(2,1)} %param.17) | copy-start | bytes 786436
  242.7 52.6 %reduce-scatter.2.cloned.1.call-start = ((), (), s32[]{:S(2)}) async-start(), calls=%async_computation.6 | async-start | bytes 786432 | tf_op jit(solution)/shard_map/reduce_scatter | solution.py:75
Sparse Core Ops, SparseCore 0:
  9.5 73.6 all-gather.10
  85.3 71.3 all-gather.6
  158.7 36.6 all-gather.12
  197.4 40.0 all-gather.8
  242.8 38.9 all-gather.14
  286.6 8.6 reduce-scatter.1
where the time goes:
time: 304 us
  waiting for transfers between devices  246 us (81%)
  matrix products  20.4 us (7%)
  blocking collectives  15.6 us (5%)
  between operations  14.3 us (5%)
  local copies, waits for them, and re-layouts  4.08 us (1%)
  other arithmetic  3.8 us (1%)
    all_gather x1, waiting for transfers between devices, body(): lax.all_gather(key_weight, 'blk', axis=0, tiled=True)  75.1 us
    all_gather x1, waiting for transfers between devices, body(): lax.all_gather(value_weight, 'blk', axis=0, tiled=True)  67.4 us
    all_gather x1, waiting for transfers between devices, body(): lax.all_gather(attn, 'blk', axis=0, tiled=True)  39.1 us
    all_gather x1, waiting for transfers between devices, body(): piece_values = lax.all_gather(values, 'blk', axis=0, tiled=True)  37 us
    all_gather x1, waiting for transfers between devices, body(): piece_keys = lax.all_gather(keys, 'blk', axis=0, tiled=True)  17.4 us
    all_gather x1, blocking collectives, body(): attend_slot_code = lax.all_gather(slot_code, 'blk', axis=0, tiled=True)  15.6 us
    reduce_scatter x1, waiting for transfers between devices, body(): lax.psum_scatter(partial_out.astype(jnp.bfloat16), 'heads', scatter_dimen...  8.15 us
  transfers between devices with their start and end apart: 6, of which 6 were waited for; matrix products, arithmetic and copies ran while one was open for 5% of the time, Pallas kernels for 0%

commit v1 on v0

v1 whole, which is shorter than its diff:
```python
import functools
import math

import jax
import jax.numpy as jnp
from jax import lax
from jax.experimental import pallas as pl
from jax.experimental.pallas import tpu as pltpu
from jax.sharding import PartitionSpec as P

HD = 128
F32 = jnp.float32
BF16 = jnp.bfloat16
MESH = pl.DeviceIdType.MESH


def kernel(
    nb,
    chunks,
    feats,
    kw,
    vw,
    gain,
    codes,
    queries,
    rowimg,
    hidden,
    wout,
    gate,
    out,
    wbuf,
    fown,
    fnbr,
    acc_own,
    acc_nbr,
    psend,
    precv,
    pbuf,
    gbuf,
    qbuf,
    qall,
    sbuf,
    mbuf,
    lbuf,
    obuf,
    agbuf,
    wov,
    part,
    xsend,
    xrecv,
    lsem,
    fsem,
    wz_send,
    wx_send,
    w_recv,
    f_send,
    ff_send,
    f_recv,
    q_sem,
    p_send,
    p_recv,
    k_send,
    kf_send,
    k_recv,
    a_send,
    af_send,
    a_recv,
    x_sem,
):
    Y = 2
    Z = nb // Y
    ZH = Z // 2
    half = nb // 2
    g = lax.axis_index("groups")
    b = lax.axis_index("blk")
    c = lax.axis_index("heads")
    z = b // Y
    y = b % Y
    h = z // ZH
    r = (z % ZH) * Y + y
    gp = g % 2
    gx = g + 1 - 2 * gp
    tok, dv = feats.shape
    S, kc = kw.shape
    rows, qc = queries.shape
    gc = qc // 2
    qpk = gc // HD
    R2 = 2 * rows
    CR = S // chunks
    ybro = {"blk": z * Y + 1 - y}
    xbro = {"groups": gx}
    cbro = {"heads": 1 - c}
    qbro = (1 - h) * half + r
    pending = []

    def remote(src, dst, ssem, rsem, dev):
        return pltpu.make_async_remote_copy(
            src_ref=src, dst_ref=dst, send_sem=ssem, recv_sem=rsem, device_id=dev, device_id_type=MESH
        )

    def send(cond, *args):
        copy = remote(*args)
        if cond is None:
            copy.start()
        else:
            pl.when(cond)(lambda: copy.start())
        pending.append((cond, copy))

    def arrived(ref, sem):
        pltpu.make_async_copy(ref, ref, sem).wait()

    own_k = pltpu.make_async_copy(kw, wbuf.at[0, z], lsem.at[0])
    own_v = pltpu.make_async_copy(vw, wbuf.at[1, z], lsem.at[1])
    own_k.start()
    own_v.start()

    barrier = pltpu.get_barrier_semaphore()
    for zd in range(Z):

        @pl.when(zd != z)
        def _():
            pl.semaphore_signal(barrier, inc=1, device_id={"blk": zd * Y + y}, device_id_type=MESH)

    for dev in (ybro, xbro, cbro):
        pl.semaphore_signal(barrier, inc=1, device_id=dev, device_id_type=MESH)
    own_k.wait()
    own_v.wait()
    pl.semaphore_wait(barrier, Z + 2)

    def wslot(kv, zi, ci):
        return wbuf.at[kv, zi, pl.ds(ci * CR, CR), :]

    for ci in range(chunks):
        for dirn, ok in ((1, z + 1 < Z), (-1, z >= 1)):
            slot = wslot(gp, z, ci)
            send(
                ok,
                slot,
                slot,
                wz_send.at[z, ci, (1 - dirn) // 2],
                w_recv.at[gp, z, ci],
                {"blk": b + dirn * Y},
            )

    FB = Z // 2
    for i in range(FB):
        zi = 2 * i + c
        send(
            None,
            feats.at[:, pl.ds(pl.multiple_of((zi * Y + 1 - y) * S, S), S)],
            fnbr.at[zi],
            f_send.at[i],
            f_recv.at[zi],
            ybro,
        )
    send(
        None,
        queries.at[:, pl.ds(pl.multiple_of((1 - h) * gc, gc), gc)],
        qbuf.at[h],
        q_sem.at[0],
        q_sem.at[1],
        {"blk": qbro},
    )
    floc = []
    for zi in range(Z):
        cp = pltpu.make_async_copy(
            feats.at[:, pl.ds(pl.multiple_of((zi * Y + y) * S, S), S)], fown.at[zi], fsem.at[zi]
        )
        cp.start()
        floc.append(cp)
    qloc = pltpu.make_async_copy(
        queries.at[:, pl.ds(pl.multiple_of(h * gc, gc), gc)], qbuf.at[h], lsem.at[2]
    )
    qloc.start()
    woloc = pltpu.make_async_copy(wout, wov, lsem.at[3])
    woloc.start()

    acc_own[...] = jnp.zeros_like(acc_own)
    acc_nbr[...] = jnp.zeros_like(acc_nbr)

    def mm(acc, feat, zi):
        for kv in range(2):
            acc[:, kv * kc : (kv + 1) * kc] += jnp.dot(
                feat[zi], wbuf[kv, zi], preferred_element_type=F32
            )

    for cp in floc:
        cp.wait()

    def sides(s):
        return ((z - s, z - s >= 0, -1), (z + s, z + s < Z, 1))

    for s in range(1, Z):
        for ci in range(chunks):
            for zi, ok, side in sides(s):
                slot = wslot(gp, zi, ci)
                pl.when(ok)(lambda: arrived(slot, w_recv.at[gp, zi, ci]))
                onward = b - side * Y
                more = ok & ((z + 1 < Z) if side < 0 else (z >= 1))
                send(more, slot, slot, wz_send.at[zi, ci, 0], w_recv.at[gp, zi, ci], {"blk": onward})
                send(ok, slot, slot, wx_send.at[zi, ci], w_recv.at[gp, zi, ci], xbro)
        if s - 1 < FB:
            zi = 2 * (s - 1) + c
            arrived(fnbr.at[zi], f_recv.at[zi])
            send(None, fnbr.at[zi], fnbr.at[zi], ff_send.at[s - 1], f_recv.at[zi], cbro)
        if s == 1:
            mm(acc_own, fown, z)
        else:
            for zi, ok, _ in sides(s - 1):

                @pl.when(ok)
                def _():
                    for ci in range(chunks):
                        arrived(wslot(1 - gp, zi, ci), w_recv.at[1 - gp, zi, ci])
                    mm(acc_own, fown, zi)

    for i in range(FB):
        zi = 2 * i + 1 - c
        arrived(fnbr.at[zi], f_recv.at[zi])
    for zi, ok, _ in sides(Z - 1):

        @pl.when(ok)
        def _():
            for ci in range(chunks):
                arrived(wslot(1 - gp, zi, ci), w_recv.at[1 - gp, zi, ci])

    @pl.loop(0, Z)
    def _(zi):
        mm(acc_nbr, fnbr, zi)

    psend[...] = acc_nbr[...].astype(BF16)
    send(None, psend, precv, p_send, p_recv, ybro)
    for zi, ok, _ in sides(Z - 1):
        pl.when(ok)(lambda: mm(acc_own, fown, zi))
    arrived(precv, p_recv)

    total = acc_own[...] + precv[...].astype(F32)
    for hh in range(2):
        kr = total[:, hh * HD : (hh + 1) * HD]
        scale = lax.rsqrt(jnp.mean(kr * kr, axis=-1, keepdims=True) + 1e-05)
        pbuf[hh, 0:tok, :] = (kr * scale * gain[...]).astype(BF16)
        pbuf[hh, tok : 2 * tok, :] = total[:, kc + hh * HD : kc + (hh + 1) * HD].astype(BF16)
        pbuf[hh, 2 * tok :, :] = codes[...]
    gbuf[b] = pbuf[h]
    for zd in range(Z):
        send(
            zd != z,
            pbuf.at[zd // ZH],
            gbuf.at[b],
            k_send.at[zd],
            k_recv.at[b],
            {"blk": zd * Y + y},
        )

    def collect(slot_of, fsend, recv):
        for s in range(Z):
            for zi, ok, _ in sides(s)[: 1 if s == 0 else 2]:
                bi = zi * Y + y
                if s > 0:
                    pl.when(ok)(lambda: arrived(slot_of(bi), recv.at[bi]))
                send(
                    None if s == 0 else ok, slot_of(bi), slot_of(bi), fsend.at[zi], recv.at[bi], ybro
                )
        for zi in range(Z):
            bi = zi * Y + 1 - y
            arrived(slot_of(bi), recv.at[bi])

    collect(lambda bi: gbuf.at[bi], kf_send, k_recv)

    qloc.wait()
    arrived(qbuf.at[1 - h], q_sem.at[1])
    for j in range(qpk):
        for so in range(2):
            at = j * R2 + so * rows
            qall[at : at + rows, :] = qbuf[so, :, j * HD : (j + 1) * HD]
    mbuf[...] = jnp.full_like(mbuf, -1e30)
    lbuf[...] = jnp.zeros_like(lbuf)
    obuf[...] = jnp.zeros_like(obuf)
    score_scale = 1.0 / math.sqrt(HD)

    @pl.loop(0, nb)
    def _(bi):
        code = gbuf[bi, 2 * tok :, :].astype(F32)
        img = jnp.concatenate([rowimg[...]] * qpk, axis=0)
        for t in range(tok // HD):
            s = (
                lax.dot_general(
                    qall[...],
                    gbuf[bi, t * HD : (t + 1) * HD, :],
                    (((1,), (1,)), ((), ())),
                    preferred_element_type=F32,
                )
                * score_scale
            )
            crow = code[t : t + 1, :]
            s = jnp.where((crow >= 0.0) & (crow <= img), s, -1e30)
            sbuf[bi, t] = s
            mbuf[...] = jnp.maximum(mbuf[...], s)

    mbuf[...] = jnp.broadcast_to(jnp.max(mbuf[...], axis=1, keepdims=True), mbuf.shape)

    @pl.loop(0, nb)
    def _(bi):
        top = mbuf[...]
        ps = [jnp.exp(sbuf[bi, t] - top) for t in range(tok // HD)]
        for p in ps:
            lbuf[...] += p
        obuf[...] += jnp.dot(
            jnp.concatenate([p.astype(BF16) for p in ps], axis=1),
            gbuf[bi, tok : 2 * tok, :],
            preferred_element_type=F32,
        )

    attn = (obuf[...] / jnp.sum(lbuf[...], axis=1, keepdims=True)).astype(BF16)
    for j in range(qpk):
        for so in range(2):
            at = j * R2 + so * rows
            agbuf[h, so, r, :, j * HD : (j + 1) * HD] = attn[at : at + rows, :]

    def aslot(bi):
        zz = bi // Y
        return agbuf.at[zz // ZH, :, (zz % ZH) * Y + bi % Y]

    for zd in range(Z):
        send(zd != z, aslot(b), aslot(b), a_send.at[zd], a_recv.at[b], {"blk": zd * Y + y})
    collect(aslot, af_send, a_recv)

    woloc.wait()
    hrows = half * rows

    def proj(so):
        a0 = agbuf[0, so].reshape(hrows, gc)
        a1 = agbuf[1, so].reshape(hrows, gc)
        return jnp.dot(a0, wov[0:gc, :], preferred_element_type=F32) + jnp.dot(
            a1, wov[gc:, :], preferred_element_type=F32
        )

    xsend[...] = proj(1 - c).astype(BF16)
    send(None, xsend, xrecv, x_sem.at[0], x_sem.at[1], cbro)
    part[...] = proj(c)
    arrived(xrecv, x_sem.at[1])
    out[...] = (
        hidden[...].astype(F32) + jnp.tanh(gate[0:1, 0:1]) * (part[...] + xrecv[...].astype(F32))
    ).astype(BF16)

    for cond, copy in pending:
        if cond is None:
            copy.wait_send()
        else:
            pl.when(cond)(lambda: copy.wait_send())


def body(
    nb,
    image_feats,
    slot_image,
    key_weight,
    value_weight,
    key_gain,
    queries,
    text_image,
    text_hidden,
    out_weight,
    attn_gate,
):
    Z = nb // 2
    ZH = Z // 2
    half = nb // 2
    tok, dv = image_feats.shape
    S, kc = key_weight.shape
    rows, qc = queries.shape
    gc = qc // 2
    qpk = gc // HD
    M = qpk * 2 * rows
    trows, ocols = text_hidden.shape
    chunks = 4
    b = lax.axis_index("blk")
    r = b % half
    img = text_image.astype(F32).reshape(2, half, rows)
    img = lax.dynamic_index_in_dim(img, r, 1, keepdims=False).reshape(2 * rows, 1)
    rowimg = jnp.broadcast_to(img, (2 * rows, HD))
    codes = jnp.pad(
        slot_image.astype(BF16).reshape(tok // HD, HD),
        ((0, 16 - tok // HD), (0, 0)),
        constant_values=-1,
    )
    gate = jnp.broadcast_to(attn_gate.reshape(1, 1), (1, HD))
    pay = 2 * tok + 16
    any_spec = pl.BlockSpec(memory_space=pl.ANY)
    vspec = pl.BlockSpec(memory_space=pltpu.VMEM)
    dma = pltpu.SemaphoreType.DMA
    V = pltpu.VMEM
    return pl.pallas_call(
        functools.partial(kernel, nb, chunks),
        out_shape=jax.ShapeDtypeStruct((trows, ocols), BF16),
        in_specs=[
            any_spec,
            any_spec,
            any_spec,
            vspec,
            vspec,
            any_spec,
            vspec,
            vspec,
            any_spec,
            vspec,
        ],
        out_specs=vspec,
        scratch_shapes=[
            V((2, Z, S, kc), BF16),
            V((Z, tok, S), BF16),
            V((Z, tok, S), BF16),
            V((tok, 2 * kc), F32),
            V((tok, 2 * kc), F32),
            V((tok, 2 * kc), BF16),
            V((tok, 2 * kc), BF16),
            V((2, pay, HD), BF16),
            V((nb, pay, HD), BF16),
            V((2, rows, gc), BF16),
            V((M, HD), BF16),
            V((nb, tok // HD, M, HD), F32),
            V((M, HD), F32),
            V((M, HD), F32),
            V((M, HD), F32),
            V((2, 2, half, rows, gc), BF16),
            V(out_weight.shape, BF16),
            V((trows, ocols), F32),
            V((trows, ocols), BF16),
            V((trows, ocols), BF16),
            dma((4,)),
            dma((Z,)),
            dma((Z, chunks, 2)),
            dma((Z, chunks)),
            dma((2, Z, chunks)),
            dma((Z // 2,)),
            dma((Z // 2,)),
            dma((Z,)),
            dma((2,)),
            dma,
            dma,
            dma((Z,)),
            dma((Z,)),
            dma((nb,)),
            dma((Z,)),
            dma((Z,)),
            dma((nb,)),
            dma((2,)),
        ],
        compiler_params=pltpu.CompilerParams(
            collective_id=0, has_side_effects=True, vmem_limit_bytes=60 * 1024 * 1024
        ),
    )(
        image_feats,
        key_weight,
        value_weight,
        key_gain.reshape(1, HD),
        codes,
        queries,
        rowimg,
        text_hidden,
        out_weight,
        gate,
    )


def solution(mesh):
    placed = (
        P(("groups", "blk"), None),
        P(("groups", "blk")),
        P("blk", "heads"),
        P("blk", "heads"),
        P(),
        P(("groups", "blk"), "heads"),
        P("groups"),
        P(("groups", "heads"), "blk"),
        P("heads", "blk"),
        P(),
    )
    return jax.shard_map(
        functools.partial(body, mesh.shape["blk"]),
        mesh=mesh,
        in_specs=placed,
        out_specs=P(("groups", "heads"), "blk"),
        check_vma=False,
    )
```

time: 304 us -> 98.8 us (0.33)
  waiting for transfers between devices: 246 us -> 0 us
  Pallas kernels: 0 us -> 92.9 us
  matrix products: 20.4 us -> 0 us
  blocking collectives: 15.6 us -> 0 us
  between operations: 14.3 us -> 0.66 us
    all_gather x5 -> x0, waiting for transfers between devices: 236 us -> none  [the longest x1 75.1 us: body(): lax.all_gather(key_weight, 'blk', axis=0, tiled=True)]
    pallas_call x0 -> x1, Pallas kernels: none -> 92.9 us  [body(): pl.pallas_call(functools.partial(kernel, nb, chunks), out_shape=jax.Shape...]
    dot_general x5 -> x0, matrix products: 20.4 us -> none  [the longest x1 5.35 us: body(): jnp.dot(image_feats, lax.all_gather(value_weight, 'blk', axis=0, tiled=Tr...]
    all_gather x1 -> x0, blocking collectives: 15.6 us -> none  [body(): attend_slot_code = lax.all_gather(slot_code, 'blk', axis=0, tiled=True)]
    reduce_scatter x1 -> x0, waiting for transfers between devices: 8.15 us -> none  [body(): lax.psum_scatter(partial_out.astype(jnp.bfloat16), 'heads', scatter_dimen...]
  transfers between devices with their start and end apart: 6 -> 0, of which waited for: 6 -> 0; matrix products, arithmetic and copies ran while one was open for 5% -> 0% of each run, Pallas kernels for 0% -> 0%
where the time goes in v1:
time: 98.8 us; the launch traced here: 98.6 us
  Pallas kernels  92.9 us (94%)
  local copies, waits for them, and re-layouts  3.68 us (4%)
  other arithmetic  1.36 us (1%)
    pallas_call x1, Pallas kernels, body(): pl.pallas_call(functools.partial(kernel, nb, chunks), out_shape=jax.Shape...  92.9 us

profile of v1, /device:TPU:1, one launch (start us, length us, event | category | flops | bytes accessed | tf_op | source)
XLA Modules:
  0.0 98.6 jit_solution(12806546466931338157)
XLA Ops:
  0.7 0.5 broadcast_in_dim.17.gate
  1.2 0.7 convert_bitcast_fusion
  1.9 0.7 convert_element_type.9
  2.5 0.1 reshape.18
  2.7 0.1 broadcast_in_dim.14
  2.7 0.6 pad.4.codes
  3.3 0.7 broadcast_in_dim.15.rowimg
  4.0 92.9 %shard_map.100 = bf16[128,1024]{1,0:T(8,128)(2,1)} custom-call(bf16[256,8192]{1,0:T(8,128)(2,1)} %feats.1, bf16[1024,256]{1,0:T(8,128)(2,1)} %kw.1, bf16[1024,256]{1,0:T(8,128)(2,1)} %vw.1, f32[1,128]{1,0:T(1,128)} %bitcast.5, bf16[16,128]{1,0:T(8,128)(2,1)} %pad.4.codes, bf16[32,2048]{1,0:T(8,128)(2,1)} %queries.1, f32[64,128]{1,0:T(8,128)} %broadcast_in_dim.15.rowimg, ...), custom_call_target="tpu_custom_call" | custom-call | tf_op jit(solution)/shard_map/pallas_call | solution.py:393
  96.9 1.7 %copy.13 = bf16[128,1024]{1,0:T(8,128)(2,1)} copy(bf16[128,1024]{1,0:T(8,128)(2,1)} %shard_map.100) | data formatting | bytes 524288
  (1 shorter events, 0.0 us)

commit v2 on v1

--- a/solution.py
+++ b/solution.py
@@ -21,9 +21,9 @@
     kw,
     vw,
     gain,
-    codes,
+    slots,
     queries,
-    rowimg,
+    text,
     hidden,
     wout,
     gate,
@@ -41,8 +41,7 @@
     qall,
     sbuf,
     mbuf,
-    lbuf,
-    obuf,
+    img,
     agbuf,
     wov,
     part,
@@ -62,7 +61,7 @@
     k_send,
     kf_send,
     k_recv,
-    a_send,
+    az_send,
     af_send,
     a_recv,
     x_sem,
@@ -224,48 +223,43 @@
             for ci in range(chunks):
                 arrived(wslot(1 - gp, zi, ci), w_recv.at[1 - gp, zi, ci])
 
-    @pl.loop(0, Z)
-    def _(zi):
-        mm(acc_nbr, fnbr, zi)
-
-    psend[...] = acc_nbr[...].astype(BF16)
-    send(None, psend, precv, p_send, p_recv, ybro)
+    TC = tok // HD
+    for t in range(TC):
+        lo, hi = t * HD, (t + 1) * HD
+
+        @pl.loop(0, Z)
+        def _(zi):
+            for kv in range(2):
+                acc_nbr[lo:hi, kv * kc : (kv + 1) * kc] += jnp.dot(
+                    fnbr[zi, lo:hi, :], wbuf[kv, zi], preferred_element_type=F32
+                )
+
+        psend[t] = acc_nbr[lo:hi, :].astype(BF16)
+        send(None, psend.at[t], precv.at[t], p_send.at[t], p_recv.at[t], ybro)
     for zi, ok, _ in sides(Z - 1):
         pl.when(ok)(lambda: mm(acc_own, fown, zi))
-    arrived(precv, p_recv)
-
-    total = acc_own[...] + precv[...].astype(F32)
-    for hh in range(2):
-        kr = total[:, hh * HD : (hh + 1) * HD]
-        scale = lax.rsqrt(jnp.mean(kr * kr, axis=-1, keepdims=True) + 1e-05)
-        pbuf[hh, 0:tok, :] = (kr * scale * gain[...]).astype(BF16)
-        pbuf[hh, tok : 2 * tok, :] = total[:, kc + hh * HD : kc + (hh + 1) * HD].astype(BF16)
-        pbuf[hh, 2 * tok :, :] = codes[...]
-    gbuf[b] = pbuf[h]
-    for zd in range(Z):
-        send(
-            zd != z,
-            pbuf.at[zd // ZH],
-            gbuf.at[b],
-            k_send.at[zd],
-            k_recv.at[b],
-            {"blk": zd * Y + y},
-        )
-
-    def collect(slot_of, fsend, recv):
-        for s in range(Z):
-            for zi, ok, _ in sides(s)[: 1 if s == 0 else 2]:
-                bi = zi * Y + y
-                if s > 0:
-                    pl.when(ok)(lambda: arrived(slot_of(bi), recv.at[bi]))
-                send(
-                    None if s == 0 else ok, slot_of(bi), slot_of(bi), fsend.at[zi], recv.at[bi], ybro
-                )
-        for zi in range(Z):
-            bi = zi * Y + 1 - y
-            arrived(slot_of(bi), recv.at[bi])
-
-    collect(lambda bi: gbuf.at[bi], kf_send, k_recv)
+
+    for t in range(TC):
+        arrived(precv.at[t], p_recv.at[t])
+        total = acc_own[t * HD : (t + 1) * HD, :] + precv[t].astype(F32)
+        code = jnp.broadcast_to(slots[t : t + 1, :].astype(F32), (16, HD)).astype(BF16)
+        for hh in range(2):
+            kr = total[:, hh * HD : (hh + 1) * HD]
+            scale = lax.rsqrt(jnp.mean(kr * kr, axis=-1, keepdims=True) + 1e-05)
+            pbuf[hh, t, 0:HD, :] = (kr * scale * gain[...]).astype(BF16)
+            pbuf[hh, t, HD : 2 * HD, :] = total[:, kc + hh * HD : kc + (hh + 1) * HD].astype(BF16)
+            pbuf[hh, t, 2 * HD :, :] = code
+        gbuf[b, t] = pbuf[h, t]
+        for zd in range(Z):
+            send(
+                zd != z,
+                pbuf.at[zd // ZH, t],
+                gbuf.at[b, t],
+                k_send.at[zd, t],
+                k_recv.at[b, t],
+                {"blk": zd * Y + y},
+            )
+        send(None, gbuf.at[b, t], gbuf.at[b, t], kf_send.at[z, t], k_recv.at[b, t], ybro)
 
     qloc.wait()
     arrived(qbuf.at[1 - h], q_sem.at[1])
@@ -273,74 +267,119 @@
         for so in range(2):
             at = j * R2 + so * rows
             qall[at : at + rows, :] = qbuf[so, :, j * HD : (j + 1) * HD]
+    count = text.shape[1]
+    lane = lax.broadcasted_iota(jnp.int32, (R2, count), 1)
+    sub = lax.broadcasted_iota(jnp.int32, (R2, count), 0)
+    want = jnp.where(sub < rows, sub, sub + (half - 1) * rows) + r * rows
+    picked = jnp.where(lane == want, text[...].astype(F32), 0.0)
+    rowcol = jnp.broadcast_to(jnp.sum(picked, axis=1, keepdims=True), (R2, HD))
+    for j in range(qpk):
+        img[j * R2 : (j + 1) * R2, :] = rowcol
     mbuf[...] = jnp.full_like(mbuf, -1e30)
-    lbuf[...] = jnp.zeros_like(lbuf)
-    obuf[...] = jnp.zeros_like(obuf)
     score_scale = 1.0 / math.sqrt(HD)
 
-    @pl.loop(0, nb)
-    def _(bi):
-        code = gbuf[bi, 2 * tok :, :].astype(F32)
-        img = jnp.concatenate([rowimg[...]] * qpk, axis=0)
-        for t in range(tok // HD):
+    def score(bi):
+        top = mbuf[...]
+        for t in range(TC):
             s = (
                 lax.dot_general(
                     qall[...],
-                    gbuf[bi, t * HD : (t + 1) * HD, :],
+                    gbuf[bi, t, 0:HD, :],
                     (((1,), (1,)), ((), ())),
                     preferred_element_type=F32,
                 )
                 * score_scale
             )
-            crow = code[t : t + 1, :]
-            s = jnp.where((crow >= 0.0) & (crow <= img), s, -1e30)
+            crow = gbuf[bi, t, 2 * HD :, :].astype(F32)[0:1, :]
+            s = jnp.where((crow >= 0.0) & (crow <= img[...]), s, -1e30)
             sbuf[bi, t] = s
-            mbuf[...] = jnp.maximum(mbuf[...], s)
-
-    mbuf[...] = jnp.broadcast_to(jnp.max(mbuf[...], axis=1, keepdims=True), mbuf.shape)
-
-    @pl.loop(0, nb)
-    def _(bi):
-        top = mbuf[...]
-        ps = [jnp.exp(sbuf[bi, t] - top) for t in range(tok // HD)]
-        for p in ps:
-            lbuf[...] += p
-        obuf[...] += jnp.dot(
-            jnp.concatenate([p.astype(BF16) for p in ps], axis=1),
-            gbuf[bi, tok : 2 * tok, :],
-            preferred_element_type=F32,
-        )
-
-    attn = (obuf[...] / jnp.sum(lbuf[...], axis=1, keepdims=True)).astype(BF16)
-    for j in range(qpk):
-        for so in range(2):
-            at = j * R2 + so * rows
-            agbuf[h, so, r, :, j * HD : (j + 1) * HD] = attn[at : at + rows, :]
-
-    def aslot(bi):
+            top = jnp.maximum(top, s)
+        mbuf[...] = top
+
+    for s in range(1, Z):
+        for t in range(TC):
+            for zi, ok, _ in sides(s):
+                slot = gbuf.at[zi * Y + y, t]
+                sem = k_recv.at[zi * Y + y, t]
+                pl.when(ok)(lambda: arrived(slot, sem))
+                send(ok, slot, slot, kf_send.at[zi, t], sem, ybro)
+
+    @pl.loop(0, Z)
+    def _(zi):
+        score(zi * Y + y)
+
+    @pl.loop(0, Z)
+    def _(zi):
+        for t in range(TC):
+            arrived(gbuf.at[zi * Y + 1 - y, t], k_recv.at[zi * Y + 1 - y, t])
+        score(zi * Y + 1 - y)
+
+    NC = agbuf.shape[1]
+    HC = qpk // NC
+    MC = HC * R2
+
+    def aslot(bi, jc):
         zz = bi // Y
-        return agbuf.at[zz // ZH, :, (zz % ZH) * Y + bi % Y]
-
-    for zd in range(Z):
-        send(zd != z, aslot(b), aslot(b), a_send.at[zd], a_recv.at[b], {"blk": zd * Y + y})
-    collect(aslot, af_send, a_recv)
+        return agbuf.at[zz // ZH, jc, :, (zz % ZH) * Y + bi % Y]
+
+    for jc in range(NC):
+        r0, r1 = jc * MC, (jc + 1) * MC
+        top = jnp.max(mbuf[r0:r1, :], axis=1, keepdims=True)
+
+        def step(bi, carry):
+            tot, acc = carry
+            ps = [jnp.exp(sbuf[bi, t, r0:r1, :] - top) for t in range(TC)]
+            for p in ps:
+                tot = tot + p
+            acc = acc + jnp.dot(
+                jnp.concatenate([p.astype(BF16) for p in ps], axis=1),
+                jnp.concatenate([gbuf[bi, t, HD : 2 * HD, :] for t in range(TC)], axis=0),
+                preferred_element_type=F32,
+            )
+            return tot, acc
+
+        zero = jnp.zeros((MC, HD), F32)
+        tot, acc = lax.fori_loop(0, nb, step, (zero, zero))
+        attn = (acc / jnp.sum(tot, axis=1, keepdims=True)).astype(BF16)
+        for jj in range(HC):
+            for so in range(2):
+                at = jj * R2 + so * rows
+                agbuf[h, jc, so, r, :, jj * HD : (jj + 1) * HD] = attn[at : at + rows, :]
+        slot = aslot(b, jc)
+        sem = a_recv.at[b, jc]
+        send(z + 1 < Z, slot, slot, az_send.at[z, jc, 0], sem, {"blk": b + Y})
+        send(z >= 1, slot, slot, az_send.at[z, jc, 1], sem, {"blk": b - Y})
+        send(None, slot, slot, af_send.at[z, jc], sem, ybro)
+
+    for s in range(1, Z):
+        for jc in range(NC):
+            for zi, ok, side in sides(s):
+                bi = zi * Y + y
+                slot = aslot(bi, jc)
+                sem = a_recv.at[bi, jc]
+                pl.when(ok)(lambda: arrived(slot, sem))
+                more = ok & ((z + 1 < Z) if side < 0 else (z >= 1))
+                send(more, slot, slot, az_send.at[zi, jc, 0], sem, {"blk": b - side * Y})
+                send(ok, slot, slot, af_send.at[zi, jc], sem, ybro)
+    for zi in range(Z):
+        for jc in range(NC):
+            bi = zi * Y + 1 - y
+            arrived(aslot(bi, jc), a_recv.at[bi, jc])
 
     woloc.wait()
     hrows = half * rows
+    ocols = out.shape[1]
 
     def proj(so):
-        a0 = agbuf[0, so].reshape(hrows, gc)
-        a1 = agbuf[1, so].reshape(hrows, gc)
-        return jnp.dot(a0, wov[0:gc, :], preferred_element_type=F32) + jnp.dot(
-            a1, wov[gc:, :], preferred_element_type=F32
-        )
+        a = [agbuf[hh, jc, so].reshape(hrows, HC * HD) for hh in range(2) for jc in range(NC)]
+        return jnp.dot(jnp.concatenate(a, axis=1), wov[...], preferred_element_type=F32)
 
     xsend[...] = proj(1 - c).astype(BF16)
     send(None, xsend, xrecv, x_sem.at[0], x_sem.at[1], cbro)
     part[...] = proj(c)
     arrived(xrecv, x_sem.at[1])
     out[...] = (
-        hidden[...].astype(F32) + jnp.tanh(gate[0:1, 0:1]) * (part[...] + xrecv[...].astype(F32))
+        hidden[...].astype(F32) + jnp.tanh(jnp.full((1, ocols), gate[0], F32)) * (part[...] + xrecv[...].astype(F32))
     ).astype(BF16)
 
     for cond, copy in pending:
@@ -373,19 +412,9 @@
     qpk = gc // HD
     M = qpk * 2 * rows
     trows, ocols = text_hidden.shape
-    chunks = 4
-    b = lax.axis_index("blk")
-    r = b % half
-    img = text_image.astype(F32).reshape(2, half, rows)
-    img = lax.dynamic_index_in_dim(img, r, 1, keepdims=False).reshape(2 * rows, 1)
-    rowimg = jnp.broadcast_to(img, (2 * rows, HD))
-    codes = jnp.pad(
-        slot_image.astype(BF16).reshape(tok // HD, HD),
-        ((0, 16 - tok // HD), (0, 0)),
-        constant_values=-1,
-    )
-    gate = jnp.broadcast_to(attn_gate.reshape(1, 1), (1, HD))
-    pay = 2 * tok + 16
+    chunks = 8 if S % 128 == 0 else 4
+    TC = tok // HD
+    NC = max(1, qpk // 2)
     any_spec = pl.BlockSpec(memory_space=pl.ANY)
     vspec = pl.BlockSpec(memory_space=pltpu.VMEM)
     dma = pltpu.SemaphoreType.DMA
@@ -403,7 +432,7 @@
             vspec,
             vspec,
             any_spec,
-            vspec,
+            pl.BlockSpec(memory_space=pltpu.SMEM),
         ],
         out_specs=vspec,
         scratch_shapes=[
@@ -412,17 +441,16 @@
             V((Z, tok, S), BF16),
             V((tok, 2 * kc), F32),
             V((tok, 2 * kc), F32),
-            V((tok, 2 * kc), BF16),
-            V((tok, 2 * kc), BF16),
-            V((2, pay, HD), BF16),
-            V((nb, pay, HD), BF16),
+            V((TC, HD, 2 * kc), BF16),
+            V((TC, HD, 2 * kc), BF16),
+            V((2, TC, 2 * HD + 16, HD), BF16),
+            V((nb, TC, 2 * HD + 16, HD), BF16),
             V((2, rows, gc), BF16),
             V((M, HD), BF16),
             V((nb, tok // HD, M, HD), F32),
             V((M, HD), F32),
             V((M, HD), F32),
-            V((M, HD), F32),
-            V((2, 2, half, rows, gc), BF16),
+            V((2, NC, 2, half, rows, gc // NC), BF16),
             V(out_weight.shape, BF16),
             V((trows, ocols), F32),
             V((trows, ocols), BF16),
@@ -436,14 +464,14 @@
             dma((Z // 2,)),
             dma((Z,)),
             dma((2,)),
-            dma,
-            dma,
-            dma((Z,)),
-            dma((Z,)),
-            dma((nb,)),
-            dma((Z,)),
-            dma((Z,)),
-            dma((nb,)),
+            dma((TC,)),
+            dma((TC,)),
+            dma((Z, TC)),
+            dma((Z, TC)),
+            dma((nb, TC)),
+            dma((Z, NC, 2)),
+            dma((Z, NC)),
+            dma((nb, NC)),
             dma((2,)),
         ],
         compiler_params=pltpu.CompilerParams(
@@ -454,12 +482,12 @@
         key_weight,
         value_weight,
         key_gain.reshape(1, HD),
-        codes,
+        slot_image.reshape(TC, HD),
         queries,
-        rowimg,
+        text_image.reshape(1, text_image.shape[0]),
         text_hidden,
         out_weight,
-        gate,
+        attn_gate,
     )
 
 

time: 98.8 us -> 93.8 us (0.949)
  local copies, waits for them, and re-layouts: 3.68 us -> 1.67 us
  Pallas kernels: 92.9 us -> 91.3 us
  other arithmetic: 1.36 us -> 0 us
    pallas_call x1, Pallas kernels: 92.9 us -> 91.3 us  [body(): pl.pallas_call(functools.partial(kernel, nb, chunks), out_shape=jax.Shape...]
    broadcast_in_dim x3 -> x0, local copies, waits for them, and re-layouts: 1.31 us -> none  [the longest x2 0.77 us: body(): rowimg = jnp.broadcast_to(img, (2 * rows, HD))]
where the time goes in v2:
time: 93.8 us; the launch traced here: 93.6 us
  Pallas kernels  91.3 us (97%)
  local copies, waits for them, and re-layouts  1.67 us (2%)
    pallas_call x1, Pallas kernels, body(): pl.pallas_call(functools.partial(kernel, nb, chunks), out_shape=jax.Shape...  91.3 us

profile of v2, /device:TPU:1, one launch (start us, length us, event | category | flops | bytes accessed | tf_op | source)
XLA Modules:
  0.0 93.6 jit_solution(11814023772644961619)
XLA Ops:
  0.7 91.3 %shard_map.100 = bf16[128,1024]{1,0:T(8,128)(2,1)} custom-call(bf16[256,8192]{1,0:T(8,128)(2,1)} %feats.1, bf16[1024,256]{1,0:T(8,128)(2,1)} %kw.1, bf16[1024,256]{1,0:T(8,128)(2,1)} %vw.1, f32[1,128]{1,0:T(1,128)} %bitcast.5, s32[2,128]{1,0:T(2,128)} %bitcast.3, bf16[32,2048]{1,0:T(8,128)(2,1)} %queries.1, s32[1,256]{1,0:T(1,128)} %bitcast.4, ...), custom_call_target="tpu_custom_call" | custom-call | tf_op jit(solution)/shard_map/pallas_call | solution.py:422
  91.9 1.7 %copy.13 = bf16[128,1024]{1,0:T(8,128)(2,1)} copy(bf16[128,1024]{1,0:T(8,128)(2,1)} %shard_map.100) | data formatting | bytes 524288

commit v3 on v2

--- a/solution.py
+++ b/solution.py
@@ -65,6 +65,8 @@
     af_send,
     a_recv,
     x_sem,
+    hid,
+    h_sem,
 ):
     Y = 2
     Z = nb // Y
@@ -173,6 +175,8 @@
     qloc.start()
     woloc = pltpu.make_async_copy(wout, wov, lsem.at[3])
     woloc.start()
+    hloc = pltpu.make_async_copy(hidden, hid, h_sem)
+    hloc.start()
 
     acc_own[...] = jnp.zeros_like(acc_own)
     acc_nbr[...] = jnp.zeros_like(acc_nbr)
@@ -367,6 +371,7 @@
             arrived(aslot(bi, jc), a_recv.at[bi, jc])
 
     woloc.wait()
+    hloc.wait()
     hrows = half * rows
     ocols = out.shape[1]
 
@@ -379,7 +384,7 @@
     part[...] = proj(c)
     arrived(xrecv, x_sem.at[1])
     out[...] = (
-        hidden[...].astype(F32) + jnp.tanh(jnp.full((1, ocols), gate[0], F32)) * (part[...] + xrecv[...].astype(F32))
+        hid[...].astype(F32) + jnp.tanh(jnp.full((1, ocols), gate[0], F32)) * (part[...] + xrecv[...].astype(F32))
     ).astype(BF16)
 
     for cond, copy in pending:
@@ -430,7 +435,7 @@
             vspec,
             any_spec,
             vspec,
-            vspec,
+            any_spec,
             any_spec,
             pl.BlockSpec(memory_space=pltpu.SMEM),
         ],
@@ -473,6 +478,8 @@
             dma((Z, NC)),
             dma((nb, NC)),
             dma((2,)),
+            V((trows, ocols), BF16),
+            dma,
         ],
         compiler_params=pltpu.CompilerParams(
             collective_id=0, has_side_effects=True, vmem_limit_bytes=60 * 1024 * 1024

time: 93.8 us -> 93.5 us (level)
  no operation moved by 1% of the time
where the time goes in v3:
time: 93.5 us; the launch traced here: 93.3 us
  Pallas kernels  91 us (97%)
  local copies, waits for them, and re-layouts  1.67 us (2%)
    pallas_call x1, Pallas kernels, body(): pl.pallas_call(functools.partial(kernel, nb, chunks), out_shape=jax.Shape...  91 us

profile of v3, /device:TPU:1, one launch (start us, length us, event | category | flops | bytes accessed | tf_op | source)
XLA Modules:
  0.0 93.3 jit_solution(14803790024741946863)
XLA Ops:
  0.7 91.0 %shard_map.100 = bf16[128,1024]{1,0:T(8,128)(2,1)} custom-call(bf16[256,8192]{1,0:T(8,128)(2,1)} %feats.1, bf16[1024,256]{1,0:T(8,128)(2,1)} %kw.1, bf16[1024,256]{1,0:T(8,128)(2,1)} %vw.1, f32[1,128]{1,0:T(1,128)} %bitcast.5, s32[2,128]{1,0:T(2,128)} %bitcast.3, bf16[32,2048]{1,0:T(8,128)(2,1)} %queries.1, s32[1,256]{1,0:T(1,128)} %bitcast.4, ...), custom_call_target="tpu_custom_call" | custom-call | tf_op jit(solution)/shard_map/pallas_call | solution.py:427
  91.7 1.7 %copy.13 = bf16[128,1024]{1,0:T(8,128)(2,1)} copy(bf16[128,1024]{1,0:T(8,128)(2,1)} %shard_map.100) | data formatting | bytes 524288
